TPU v7x, 32 devices: a whole 2x2x4 slice. The times are simulated.
32 devices in a mesh: band: 8 (over z, core), grid: 4 (over y, x).
Axes of the slice: x: 2, y: 2, z: 4, core: 2. Of those that a mesh axis runs over, the one named last changes fastest.
Arguments:
- orbitals: bfloat16 [16, 192, 192, 192], P('band', 'grid'), may hold values from -6 to 6
- plan: int32 [2, 16], P(None, 'band'), may hold values from 0 to 1
Outputs:
- exchange_image: bfloat16 [16, 192, 192, 192], P('band', 'grid')
Inputs may be any that keep to these rules, and one draw needn't show every extreme that they name: plan[s, i] is the position, within the partner group of band i at shift s + 1, of the band that band i pairs with.
All inputs are finite; a program needn't handle non-finite values.
Results may differ from a plain program's by a relative error of at most 0.0095.
Values may be sent and summed in bfloat16 or wider, within the bound.
A program may use at most 192 MiB of HBM per device.

v0:
```python
import jax
import jax.numpy as jnp
from jax import lax
from jax.sharding import PartitionSpec as P

SHIFTS = 2
screening = 0.0005


def shifted(block, axis, distance):
    devices = range(lax.axis_size(axis))
    route = [((i - distance) % len(devices), i) for i in devices]
    return lax.ppermute(block, axis, route)


def sine_table(length):
    counts = jnp.arange(1, length + 1, dtype=jnp.float32)
    return jnp.sin(jnp.pi * counts[:, None] * counts[None, :] / (length + 1)).astype(jnp.bfloat16)


def eigen_line(modes, length):
    return 2.0 - 2.0 * jnp.cos(jnp.pi * modes / (length + 1))


def shards(orbitals, plan):
    per_group, slab_planes, _, length = orbitals.shape
    columns = length // lax.axis_size("grid")
    sines = sine_table(length)
    modes = jnp.arange(1, length + 1, dtype=jnp.float32)
    local_modes = (
        lax.axis_index("grid") * columns + jnp.arange(1, columns + 1, dtype=jnp.int32)
    ).astype(jnp.float32)
    along_full = eigen_line(modes, length)
    along_local = eigen_line(local_modes, length)
    kernel = (2.0 / (length + 1)) ** 3 / (
        along_full[:, None, None]
        + along_local[None, :, None]
        + along_full[None, None, :]
        + screening
    )
    positions = jnp.arange(per_group, dtype=jnp.int32)
    own_sums = jnp.zeros(orbitals.shape, jnp.float32)
    for offset in range(1, SHIFTS + 1):
        partner_block = shifted(orbitals, "band", -offset)
        picker = (plan[offset - 1][:, None] == positions[None, :]).astype(jnp.bfloat16)
        chosen = jnp.einsum(
            "ip,pxyz->ixyz", picker, partner_block, preferred_element_type=jnp.float32
        ).astype(jnp.bfloat16)
        density = (orbitals.astype(jnp.float32) * chosen.astype(jnp.float32)).astype(jnp.bfloat16)
        section = jnp.dot(density, sines, preferred_element_type=jnp.float32).astype(jnp.bfloat16)
        section = jnp.einsum(
            "pxyz,ky->pxkz", section, sines, preferred_element_type=jnp.float32
        ).astype(jnp.bfloat16)
        spectrum = jnp.einsum(
            "pxyz,kx->pkyz",
            lax.all_to_all(section, "grid", split_axis=2, concat_axis=1, tiled=True),
            sines,
            preferred_element_type=jnp.float32,
        )
        scaled = (spectrum * kernel).astype(jnp.bfloat16)
        inverse = jnp.einsum(
            "pxyz,kx->pkyz", scaled, sines, preferred_element_type=jnp.float32
        ).astype(jnp.bfloat16)
        planes = jnp.einsum(
            "pxyz,ky->pxkz",
            lax.all_to_all(inverse, "grid", split_axis=1, concat_axis=2, tiled=True),
            sines,
            preferred_element_type=jnp.float32,
        ).astype(jnp.bfloat16)
        potential = jnp.dot(planes, sines, preferred_element_type=jnp.float32)
        own_term = potential * chosen.astype(jnp.float32)
        weighted = potential * orbitals.astype(jnp.float32)
        partner_term = jnp.einsum(
            "ip,ixyz->pxyz", picker.astype(jnp.float32), weighted, precision=lax.Precision.HIGHEST
        )
        own_term, partner_term = (own_term, partner_term)
        own_sums = own_sums + own_term
        returned = shifted(partner_term.astype(jnp.bfloat16), "band", offset)
        own_sums = own_sums + returned.astype(jnp.float32)
    return (-own_sums).astype(jnp.bfloat16)


def solution(mesh):
    return jax.shard_map(
        shards,
        mesh=mesh,
        in_specs=(P("band", "grid", None, None), P(None, "band")),
        out_specs=P("band", "grid", None, None),
        check_vma=False,
    )
```

profile of v0, /device:TPU:0, one launch (start us, length us, event | category | flops | bytes accessed | tf_op | source)
XLA Modules:
  0.0 1214.4 jit_solution(12034143865513514143)
XLA Ops:
  0.0 0.0 copy-start
  0.0 18.3 %copy.71 = bf16[2,48,192,192]{3,0,2,1:T(2,128)(2,1)} copy(bf16[2,48,192,192]{3,2,1,0:T(8,128)(2,1)} %param.2) | data formatting | bytes 14155776 | tf_op args[0]
  18.3 5.1 collective-permute-start.2
  23.4 0.0 collective-permute-start
  23.4 0.0 copy-done
  23.5 0.0 copy-start.1
  23.5 202.5 %collective-permute-done.2 = bf16[2,48,192,192]{3,0,2,1:T(2,128)(2,1)S(1)} collective-permute-done((bf16[2,48,192,192]{3,0,2,1:T(2,128)(2,1)}, bf16[2,48,192,192]{3,0,2,1:T(2,128)(2,1)S(1)}, u32[]{:S(2)}, u32[]{:S(2)}) %collective-permute-start.2) | collective-permute-done | bytes 7077920 | tf_op jit(solution)/shard_map/ppermute | solution.py:13
  225.9 14.5 %fusion.122 = bf16[2,48,192,192]{3,0,2,1:T(2,128)(2,1)} fusion(bf16[2,48,192,192]{3,0,2,1:T(2,128)(2,1)S(1)} %collective-permute-done.2, s32[2]{0:T(128)S(1)} %get-tuple-element.7), kind=kOutput, calls=%fused_computation.75 | convolution fusion | flops 14155780 | bytes 14155784 | tf_op jit(solution)/shard_map/ip,pxyz->ixyz/dot_general | solution.py:46
  240.4 0.0 copy-done.1
  240.4 15.2 %convert_bitcast_fusion.1 = bf16[2,48,192,192]{3,2,1,0:T(8,128)(2,1)} fusion(bf16[2,48,192,192]{3,2,1,0:T(8,128)(2,1)} %param.2, bf16[2,48,192,192]{3,0,2,1:T(2,128)(2,1)} %fusion.122, f32[192]{0:T(256)S(1)} %get-tuple-element.10, f32[192]{0:T(256)S(1)} %get-tuple-element.11), kind=kOutput, calls=%fused_computation.39 | convolution fusion | flops 2739363840 | bytes 21235200 | tf_op jit(solution)/shard_map/pxyz,ky->pxkz/dot_general | solution.py:51
  255.7 12.7 %copy.86 = bf16[2,48,192,192]{3,1,0,2:T(8,128)(2,1)} copy(bf16[2,48,192,192]{3,2,1,0:T(8,128)(2,1)} %convert_bitcast_fusion.1) | data formatting | bytes 14155776 | tf_op jit(solution)/shard_map/convert_element_type | solution.py:53
  268.4 6.0 all-to-all-start.2
  274.4 52.6 %collective-permute-done = bf16[2,48,192,192]{3,0,2,1:T(2,128)(2,1)} collective-permute-done((bf16[2,48,192,192]{3,0,2,1:T(2,128)(2,1)}, bf16[2,48,192,192]{3,0,2,1:T(2,128)(2,1)}, u32[]{:S(2)}, u32[]{:S(2)}) %collective-permute-start) | collective-permute-done | bytes 7077920 | tf_op jit(solution)/shard_map/ppermute | solution.py:13
  327.0 16.1 %fusion.123 = bf16[2,48,192,192]{3,0,2,1:T(2,128)(2,1)} fusion(bf16[2,48,192,192]{3,0,2,1:T(2,128)(2,1)} %collective-permute-done, s32[2]{0:T(128)S(1)} %get-tuple-element.8), kind=kOutput, calls=%fused_computation.77 | convolution fusion | flops 14155780 | bytes 14155784 | tf_op jit(solution)/shard_map/ip,pxyz->ixyz/dot_general | solution.py:46
  343.2 15.4 %convert_bitcast_fusion.3 = bf16[2,48,192,192]{3,2,1,0:T(8,128)(2,1)} fusion(bf16[2,48,192,192]{3,2,1,0:T(8,128)(2,1)} %param.2, bf16[2,48,192,192]{3,0,2,1:T(2,128)(2,1)} %fusion.123, f32[192]{0:T(256)S(1)} %get-tuple-element.10, f32[192]{0:T(256)S(1)} %get-tuple-element.11), kind=kOutput, calls=%fused_computation.47 | convolution fusion | flops 2739363840 | bytes 21235200 | tf_op jit(solution)/shard_map/pxyz,ky->pxkz/dot_general | solution.py:51
  358.5 12.8 %copy.74 = bf16[2,48,192,192]{3,1,0,2:T(8,128)(2,1)} copy(bf16[2,48,192,192]{3,2,1,0:T(8,128)(2,1)} %convert_bitcast_fusion.3) | data formatting | bytes 14155776 | tf_op jit(solution)/shard_map/convert_element_type | solution.py:53
  371.3 6.1 all-to-all-done.2
  377.4 6.0 all-to-all-start
  383.5 0.1 broadcast_add_fusion
  383.6 4.3 add_divide_fusion
  387.9 12.7 %copy.88 = bf16[2,4,48,48,192]{4,3,2,1,0:T(8,128)(2,1)} copy(bf16[2,4,48,48,192]{4,2,0,3,1:T(8,128)(2,1)} %bitcast.24) | data formatting | bytes 14155776 | tf_op jit(solution)/shard_map/all_to_all | solution.py:56
  400.6 16.3 %convert_bitcast_fusion = bf16[2,192,48,192]{3,1,2,0:T(8,128)(2,1)} fusion(f32[192,48,192]{2,0,1:T(8,128)} %add_divide_fusion, bf16[2,192,48,192]{3,2,1,0:T(8,128)(2,1)} %bitcast.88, f32[192]{0:T(256)S(1)} %get-tuple-element.10, f32[192]{0:T(256)S(1)} %get-tuple-element.11), kind=kOutput, calls=%fused_computation.38 | convolution fusion | flops 2728747008 | bytes 21235200 | tf_op jit(solution)/shard_map/pxyz,kx->pkyz/dot_general | solution.py:61
  416.9 12.7 %copy.90 = bf16[2,192,48,192]{3,2,0,1:T(8,128)(2,1)} copy(bf16[2,192,48,192]{3,1,2,0:T(8,128)(2,1)} %convert_bitcast_fusion) | data formatting | bytes 14155776 | tf_op jit(solution)/shard_map/convert_element_type | solution.py:63
  429.6 56.9 %all-to-all-done = bf16[2,48,192,192]{3,1,0,2:T(8,128)(2,1)} async-done(((bf16[2,48,192,192]{3,1,0,2:T(8,128)(2,1)}), bf16[2,48,192,192]{3,1,0,2:T(8,128)(2,1)}, u32[]{:S(2)}, u32[]{:S(2)}) %all-to-all-start) | async-done | bytes 7077920 | tf_op jit(solution)/shard_map/all_to_all | solution.py:56
  486.5 5.8 all-to-all-start.3
  492.3 12.7 %copy.76 = bf16[2,4,48,48,192]{4,3,2,1,0:T(8,128)(2,1)} copy(bf16[2,4,48,48,192]{4,2,0,3,1:T(8,128)(2,1)} %bitcast.8) | data formatting | bytes 14155776 | tf_op jit(solution)/shard_map/all_to_all | solution.py:56
  505.0 16.5 %convert_bitcast_fusion.2 = bf16[2,192,48,192]{3,1,2,0:T(8,128)(2,1)} fusion(f32[192,48,192]{2,0,1:T(8,128)} %add_divide_fusion, bf16[2,192,48,192]{3,2,1,0:T(8,128)(2,1)} %bitcast.87, f32[192]{0:T(256)S(1)} %get-tuple-element.10, f32[192]{0:T(256)S(1)} %get-tuple-element.11), kind=kOutput, calls=%fused_computation.43 | convolution fusion | flops 2728747008 | bytes 21235200 | tf_op jit(solution)/shard_map/pxyz,kx->pkyz/dot_general | solution.py:61
  521.6 12.7 %copy.78 = bf16[2,192,48,192]{3,2,0,1:T(8,128)(2,1)} copy(bf16[2,192,48,192]{3,1,2,0:T(8,128)(2,1)} %convert_bitcast_fusion.2) | data formatting | bytes 14155776 | tf_op jit(solution)/shard_map/convert_element_type | solution.py:63
  534.3 61.2 %all-to-all-done.3 = bf16[2,192,48,192]{3,2,0,1:T(8,128)(2,1)} async-done(((bf16[2,192,48,192]{3,2,0,1:T(8,128)(2,1)}), bf16[2,192,48,192]{3,2,0,1:T(8,128)(2,1)}, u32[]{:S(2)}, u32[]{:S(2)}) %all-to-all-start.3) | async-done | bytes 7077920 | tf_op jit(solution)/shard_map/all_to_all | solution.py:66
  595.5 5.9 all-to-all-start.1
  601.4 8.9 copy.92
  610.3 13.7 %fusion.21 = f32[2,48,192,192]{3,2,1,0:T(8,128)} fusion(bf16[2,48,192,192]{3,2,1,0:T(8,128)(2,1)} %bitcast.90, f32[192]{0:T(256)S(1)} %get-tuple-element.10, f32[192]{0:T(256)S(1)} %get-tuple-element.11), kind=kOutput, calls=%fused_computation.29 | convolution fusion | flops 2721669120 | bytes 21235200 | tf_op jit(solution)/shard_map/dot_general | solution.py:70
  624.1 80.4 %all-to-all-done.1 = bf16[2,192,48,192]{3,2,0,1:T(8,128)(2,1)} async-done(((bf16[2,192,48,192]{3,2,0,1:T(8,128)(2,1)}), bf16[2,192,48,192]{3,2,0,1:T(8,128)(2,1)}, u32[]{:S(2)}, u32[]{:S(2)}) %all-to-all-start.1) | async-done | bytes 7077920 | tf_op jit(solution)/shard_map/all_to_all | solution.py:66
  704.5 8.9 copy.80
  713.3 34.3 %convert_multiply_fusion.2 = (f32[2,48,192,192]{3,2,1,0:T(8,128)}, f32[2,48,192,192]{3,2,1,0:T(8,128)}, f32[2,48,192,192]{3,2,1,0:T(8,128)}) fusion(bf16[2,48,192,192]{3,2,1,0:T(8,128)(2,1)} %param.2, f32[2,48,192,192]{3,2,1,0:T(8,128)} %fusion.21, f32[192]{0:T(256)S(1)} %get-tuple-element.10, f32[192]{0:T(256)S(1)} %get-tuple-element.11, ...), kind=kOutput, calls=%fused_computation.2 | convolution fusion | flops 2732285952 | bytes 70780416 | tf_op jit(solution)/shard_map/dot_general | solution.py:70
  747.6 58.8 %fusion.9 = bf16[2,48,192,192]{3,0,2,1:T(2,128)(2,1)} fusion(f32[2,48,192,192]{3,2,1,0:T(8,128)} %get-tuple-element.5, s32[2]{0:T(128)S(1)} %get-tuple-element.8), kind=kOutput, calls=%fused_computation.21 | convolution fusion | flops 84934656 | bytes 21233672 | tf_op jit(solution)/shard_map/ip,ixyz->pxyz/dot_general | solution.py:73
  806.4 0.0 copy-start.2
  806.4 9.3 copy.143
  815.7 0.0 copy-done.2
  815.7 58.8 %fusion.7 = bf16[2,48,192,192]{3,0,2,1:T(2,128)(2,1)} fusion(f32[2,48,192,192]{3,2,1,0:T(8,128)} %get-tuple-element.6, s32[2]{0:T(128)S(1)} %copy-done.2), kind=kOutput, calls=%fused_computation.19 | convolution fusion | flops 84934656 | bytes 21233672 | tf_op jit(solution)/shard_map/ip,ixyz->pxyz/dot_general | solution.py:73
  874.5 9.2 copy.142
  883.8 0.3 collective-permute-start.3
  884.1 0.0 collective-permute-start.1
  884.1 207.8 %collective-permute-done.3 = bf16[2,48,192,192]{3,2,1,0:T(8,128)(2,1)S(1)} collective-permute-done((bf16[2,48,192,192]{3,2,1,0:T(8,128)(2,1)}, bf16[2,48,192,192]{3,2,1,0:T(8,128)(2,1)S(1)}, u32[]{:S(2)}, u32[]{:S(2)}) %collective-permute-start.3) | collective-permute-done | bytes 7077920 | tf_op jit(solution)/shard_map/ppermute | solution.py:13
  1091.9 99.5 %collective-permute-done.1 = bf16[2,48,192,192]{3,2,1,0:T(8,128)(2,1)S(1)} collective-permute-done((bf16[2,48,192,192]{3,2,1,0:T(8,128)(2,1)}, bf16[2,48,192,192]{3,2,1,0:T(8,128)(2,1)S(1)}, u32[]{:S(2)}, u32[]{:S(2)}) %collective-permute-start.1) | collective-permute-done | bytes 7077920 | tf_op jit(solution)/shard_map/ppermute | solution.py:13
  1191.5 22.5 %fusion.4 = bf16[2,48,192,192]{3,2,1,0:T(8,128)(2,1)} fusion(f32[2,48,192,192]{3,2,1,0:T(8,128)} %get-tuple-element.9, f32[2,48,192,192]{3,2,1,0:T(8,128)} %fusion.21, bf16[2,48,192,192]{3,2,1,0:T(8,128)(2,1)S(1)} %collective-permute-done.3, bf16[2,48,192,192]{3,2,1,0:T(8,128)(2,1)S(1)} %collective-permute-done.1, bf16[2,48,192,192]{3,0,2,1:T(2,128)(2,1)} %fusion.123, ...), kind=kLoop, calls=%fused_computation.10 | loop fusion | flops 38928384 | bytes 63700992 | tf_op jit(solution)/shard_map/convert_element_type | solution.py:80
  (4 shorter events, 0.1 us)
Async XLA Ops:
  0.0 23.4 %copy-start = (s32[2,2]{1,0:T(2,128)S(1)}, s32[2,2]{1,0:T(2,128)}, u32[]{:S(2)}) copy-start(s32[2,2]{1,0:T(2,128)} %param.3) | copy-start | bytes 52
  18.3 207.6 %collective-permute-start.2 = (bf16[2,48,192,192]{3,0,2,1:T(2,128)(2,1)}, bf16[2,48,192,192]{3,0,2,1:T(2,128)(2,1)S(1)}, u32[]{:S(2)}, u32[]{:S(2)}) collective-permute-start(bf16[2,48,192,192]{3,0,2,1:T(2,128)(2,1)} %copy.71), channel_id=1, source_target_pairs={{8,0},{12,4},{16,8},{20,12},{24,16},{28,20},{0,24},{4,28},{9,1},{1... | collective-permute-start | bytes 21233672 | tf_op jit(solution)/shard_map/ppermute | solution.py:13
  23.4 303.6 %collective-permute-start = (bf16[2,48,192,192]{3,0,2,1:T(2,128)(2,1)}, bf16[2,48,192,192]{3,0,2,1:T(2,128)(2,1)}, u32[]{:S(2)}, u32[]{:S(2)}) collective-permute-start(bf16[2,48,192,192]{3,0,2,1:T(2,128)(2,1)} %copy.71), channel_id=1, source_target_pairs={{4,0},{8,4},{12,8},{16,12},{20,16},{24,20},{28,24},{0,28},{5,1},{9... | collective-permute-start | bytes 21233672 | tf_op jit(solution)/shard_map/ppermute | solution.py:13
  23.5 217.0 %copy-start.1 = (s32[2]{0:T(128)}, s32[2]{0:T(128)S(1)}, u32[]{:S(2)}) copy-start(s32[2]{0:T(128)S(1)} %get-tuple-element.7) | copy-start | bytes 28
  268.4 109.0 %all-to-all-start.2 = ((bf16[2,48,192,192]{3,1,0,2:T(8,128)(2,1)}), bf16[2,48,192,192]{3,1,0,2:T(8,128)(2,1)}, u32[]{:S(2)}, u32[]{:S(2)}) async-start(bf16[2,48,192,192]{3,1,0,2:T(8,128)(2,1)} %copy.86), calls=%async_computation.2 | async-start | bytes 18874368 | tf_op jit(solution)/shard_map/all_to_all | solution.py:56
  377.4 109.1 %all-to-all-start = ((bf16[2,48,192,192]{3,1,0,2:T(8,128)(2,1)}), bf16[2,48,192,192]{3,1,0,2:T(8,128)(2,1)}, u32[]{:S(2)}, u32[]{:S(2)}) async-start(bf16[2,48,192,192]{3,1,0,2:T(8,128)(2,1)} %copy.74), calls=%async_computation | async-start | bytes 18874368 | tf_op jit(solution)/shard_map/all_to_all | solution.py:56
  486.5 108.9 %all-to-all-start.3 = ((bf16[2,192,48,192]{3,2,0,1:T(8,128)(2,1)}), bf16[2,192,48,192]{3,2,0,1:T(8,128)(2,1)}, u32[]{:S(2)}, u32[]{:S(2)}) async-start(bf16[2,192,48,192]{3,2,0,1:T(8,128)(2,1)} %copy.90), calls=%async_computation.3 | async-start | bytes 18874368 | tf_op jit(solution)/shard_map/all_to_all | solution.py:66
  595.5 109.0 %all-to-all-start.1 = ((bf16[2,192,48,192]{3,2,0,1:T(8,128)(2,1)}), bf16[2,192,48,192]{3,2,0,1:T(8,128)(2,1)}, u32[]{:S(2)}, u32[]{:S(2)}) async-start(bf16[2,192,48,192]{3,2,0,1:T(8,128)(2,1)} %copy.78), calls=%async_computation.1 | async-start | bytes 18874368 | tf_op jit(solution)/shard_map/all_to_all | solution.py:66
  806.4 9.3 copy-start.2
  883.8 208.2 %collective-permute-start.3 = (bf16[2,48,192,192]{3,2,1,0:T(8,128)(2,1)}, bf16[2,48,192,192]{3,2,1,0:T(8,128)(2,1)S(1)}, u32[]{:S(2)}, u32[]{:S(2)}) collective-permute-start(bf16[2,48,192,192]{3,2,1,0:T(8,128)(2,1)} %copy.142), channel_id=1, source_target_pairs={{24,0},{28,4},{0,8},{4,12},{8,16},{12,20},{16,24},{20,28},{25,1},{... | collective-permute-start | bytes 21233672 | tf_op jit(solution)/shard_map/ppermute | solution.py:13
  884.1 307.4 %collective-permute-start.1 = (bf16[2,48,192,192]{3,2,1,0:T(8,128)(2,1)}, bf16[2,48,192,192]{3,2,1,0:T(8,128)(2,1)S(1)}, u32[]{:S(2)}, u32[]{:S(2)}) collective-permute-start(bf16[2,48,192,192]{3,2,1,0:T(8,128)(2,1)} %copy.143), channel_id=1, source_target_pairs={{28,0},{0,4},{4,8},{8,12},{12,16},{16,20},{20,24},{24,28},{29,1},{... | collective-permute-start | bytes 21233672 | tf_op jit(solution)/shard_map/ppermute | solution.py:13
where the time goes:
time: 1220 us; the launch traced here: 1210 us
  waiting for transfers between devices  767 us (63%)
  matrix products  260 us (21%)
  local copies, waits for them, and re-layouts  131 us (11%)
  starting transfers between devices  29.2 us (2%)
  other arithmetic  27 us (2%)
    ppermute x4, waiting for transfers between devices, shifted(): return lax.ppermute(block, axis, route)  562 us
    all_to_all x2, waiting for transfers between devices, shards(): lax.all_to_all(inverse, 'grid', split_axis=1, concat_axis=2, tiled=True)  142 us
    dot_general x2, matrix products, shards(): jnp.einsum('ip,ixyz->pxyz', picker.astype(jnp.float32), weighted, precisi...  118 us
    all_to_all x2, waiting for transfers between devices, shards(): lax.all_to_all(section, 'grid', split_axis=2, concat_axis=1, tiled=True)  63 us
    dot_general x2, matrix products, shards(): potential = jnp.dot(planes, sines, preferred_element_type=jnp.float32)  48 us
    dot_general x2, matrix products, shards(): jnp.einsum('pxyz,kx->pkyz', scaled, sines, preferred_element_type=jnp.flo...  32.8 us
    dot_general x2, matrix products, shards(): jnp.einsum('ip,pxyz->ixyz', picker, partner_block, preferred_element_type...  30.6 us
    dot_general x2, matrix products, shards(): jnp.einsum('pxyz,ky->pxkz', section, sines, preferred_element_type=jnp.fl...  30.6 us
  transfers between devices with their start and end apart: 8, of which 8 were waited for; matrix products, arithmetic and copies ran while one was open for 16% of the time, Pallas kernels for 0%

commit v1 on v0

--- a/solution.py
+++ b/solution.py
@@ -5,6 +5,12 @@
 
 SHIFTS = 2
 screening = 0.0005
+
+
+def swap_blocks(x, mesh_axis, split, join):
+    shards = jnp.split(x, lax.axis_size(mesh_axis), axis=split)
+    got = lax.all_to_all(jnp.stack(shards), mesh_axis, 0, 0)
+    return jnp.concatenate(got, axis=join)
 
 
 def shifted(block, axis, distance):
@@ -63,7 +69,7 @@
         ).astype(jnp.bfloat16)
         planes = jnp.einsum(
             "pxyz,ky->pxkz",
-            lax.all_to_all(inverse, "grid", split_axis=1, concat_axis=2, tiled=True),
+            swap_blocks(inverse, "grid", 1, 2),
             sines,
             preferred_element_type=jnp.float32,
         ).astype(jnp.bfloat16)

time: 1220 us -> 1220 us (level)
  local copies, waits for them, and re-layouts: 131 us -> 118 us
    convert_element_type x2 -> x0, local copies, waits for them, and re-layouts: 25.4 us -> none  [shards(): inverse = jnp.einsum('pxyz,kx->pkyz', scaled, sines, preferred_element_ty...]
    reshape x0 -> x2, local copies, waits for them, and re-layouts: none -> 21.9 us  [swap_blocks(): return jnp.concatenate(got, axis=join)]
    all_to_all x2 -> x0, local copies, waits for them, and re-layouts: 17.8 us -> none  [shards(): lax.all_to_all(inverse, 'grid', split_axis=1, concat_axis=2, tiled=True)]
where the time goes in v1:
time: 1220 us
  waiting for transfers between devices  771 us (63%)
  matrix products  259 us (21%)
  local copies, waits for them, and re-layouts  118 us (10%)
  other arithmetic  38.5 us (3%)
  starting transfers between devices  30 us (2%)
    ppermute x4, waiting for transfers between devices, shifted(): return lax.ppermute(block, axis, route)  562 us
    all_to_all x2, waiting for transfers between devices, swap_blocks(): got = lax.all_to_all(jnp.stack(shards), mesh_axis, 0, 0)  143 us
    dot_general x2, matrix products, shards(): jnp.einsum('ip,ixyz->pxyz', picker.astype(jnp.float32), weighted, precisi...  118 us
    all_to_all x2, waiting for transfers between devices, shards(): lax.all_to_all(section, 'grid', split_axis=2, concat_axis=1, tiled=True)  66.5 us
    dot_general x2, matrix products, shards(): potential = jnp.dot(planes, sines, preferred_element_type=jnp.float32)  48 us
    dot_general x2, matrix products, shards(): jnp.einsum('pxyz,kx->pkyz', scaled, sines, preferred_element_type=jnp.flo...  32.4 us
    dot_general x2, matrix products, shards(): jnp.einsum('ip,pxyz->ixyz', picker, partner_block, preferred_element_type...  30.6 us
    dot_general x2, matrix products, shards(): jnp.einsum('pxyz,ky->pxkz', section, sines, preferred_element_type=jnp.fl...  30.4 us
  transfers between devices with their start and end apart: 8, of which 8 were waited for; matrix products, arithmetic and copies ran while one was open for 16% of the time, Pallas kernels for 0%

profile of v1, /device:TPU:0, one launch (start us, length us, event | category | flops | bytes accessed | tf_op | source)
XLA Modules:
  0.0 1217.3 jit_solution(7945170738966040768)
XLA Ops:
  0.0 0.0 copy-start
  0.0 18.3 %copy.67 = bf16[2,48,192,192]{3,0,2,1:T(2,128)(2,1)} copy(bf16[2,48,192,192]{3,2,1,0:T(8,128)(2,1)} %param.2) | data formatting | bytes 14155776 | tf_op args[0]
  18.3 5.1 collective-permute-start.2
  23.4 0.0 collective-permute-start
  23.4 0.0 copy-done
  23.5 0.0 copy-start.1
  23.5 202.5 %collective-permute-done.2 = bf16[2,48,192,192]{3,0,2,1:T(2,128)(2,1)S(1)} collective-permute-done((bf16[2,48,192,192]{3,0,2,1:T(2,128)(2,1)}, bf16[2,48,192,192]{3,0,2,1:T(2,128)(2,1)S(1)}, u32[]{:S(2)}, u32[]{:S(2)}) %collective-permute-start.2) | collective-permute-done | bytes 7077920 | tf_op jit(solution)/shard_map/ppermute | solution.py:19
  225.9 14.5 %fusion.122 = bf16[2,48,192,192]{3,0,2,1:T(2,128)(2,1)} fusion(bf16[2,48,192,192]{3,0,2,1:T(2,128)(2,1)S(1)} %collective-permute-done.2, s32[2]{0:T(128)S(1)} %get-tuple-element.15), kind=kOutput, calls=%fused_computation.85 | convolution fusion | flops 14155780 | bytes 14155784 | tf_op jit(solution)/shard_map/ip,pxyz->ixyz/dot_general | solution.py:52
  240.5 0.0 copy-done.1
  240.5 15.3 %convert_bitcast_fusion.1 = bf16[2,48,192,192]{3,2,1,0:T(8,128)(2,1)} fusion(bf16[2,48,192,192]{3,2,1,0:T(8,128)(2,1)} %param.2, bf16[2,48,192,192]{3,0,2,1:T(2,128)(2,1)} %fusion.122, f32[192]{0:T(256)S(1)} %get-tuple-element.18, f32[192]{0:T(256)S(1)} %get-tuple-element.19), kind=kOutput, calls=%fused_computation.41 | convolution fusion | flops 2739363840 | bytes 21235200 | tf_op jit(solution)/shard_map/pxyz,ky->pxkz/dot_general | solution.py:57
  255.8 12.7 %copy.80 = bf16[2,48,192,192]{3,1,0,2:T(8,128)(2,1)} copy(bf16[2,48,192,192]{3,2,1,0:T(8,128)(2,1)} %convert_bitcast_fusion.1) | data formatting | bytes 14155776 | tf_op jit(solution)/shard_map/convert_element_type | solution.py:59
  268.5 6.3 all-to-all-start.2
  274.8 52.2 %collective-permute-done = bf16[2,48,192,192]{3,0,2,1:T(2,128)(2,1)} collective-permute-done((bf16[2,48,192,192]{3,0,2,1:T(2,128)(2,1)}, bf16[2,48,192,192]{3,0,2,1:T(2,128)(2,1)}, u32[]{:S(2)}, u32[]{:S(2)}) %collective-permute-start) | collective-permute-done | bytes 7077920 | tf_op jit(solution)/shard_map/ppermute | solution.py:19
  327.0 16.1 %fusion.123 = bf16[2,48,192,192]{3,0,2,1:T(2,128)(2,1)} fusion(bf16[2,48,192,192]{3,0,2,1:T(2,128)(2,1)} %collective-permute-done, s32[2]{0:T(128)S(1)} %get-tuple-element.16), kind=kOutput, calls=%fused_computation.87 | convolution fusion | flops 14155780 | bytes 14155784 | tf_op jit(solution)/shard_map/ip,pxyz->ixyz/dot_general | solution.py:52
  343.2 15.1 %convert_bitcast_fusion.3 = bf16[2,48,192,192]{3,2,1,0:T(8,128)(2,1)} fusion(bf16[2,48,192,192]{3,2,1,0:T(8,128)(2,1)} %param.2, bf16[2,48,192,192]{3,0,2,1:T(2,128)(2,1)} %fusion.123, f32[192]{0:T(256)S(1)} %get-tuple-element.18, f32[192]{0:T(256)S(1)} %get-tuple-element.19), kind=kOutput, calls=%fused_computation.49 | convolution fusion | flops 2739363840 | bytes 21235200 | tf_op jit(solution)/shard_map/pxyz,ky->pxkz/dot_general | solution.py:57
  358.2 12.7 %copy.70 = bf16[2,48,192,192]{3,1,0,2:T(8,128)(2,1)} copy(bf16[2,48,192,192]{3,2,1,0:T(8,128)(2,1)} %convert_bitcast_fusion.3) | data formatting | bytes 14155776 | tf_op jit(solution)/shard_map/convert_element_type | solution.py:59
  371.0 6.9 all-to-all-done.2
  377.8 6.0 all-to-all-start
  384.0 0.1 broadcast_add_fusion
  384.0 4.3 add_divide_fusion
  388.4 12.8 %copy.82 = bf16[2,4,48,48,192]{4,3,2,1,0:T(8,128)(2,1)} copy(bf16[2,4,48,48,192]{4,2,0,3,1:T(8,128)(2,1)} %bitcast.26) | data formatting | bytes 14155776 | tf_op jit(solution)/shard_map/all_to_all | solution.py:62
  401.2 16.2 %convert_bitcast_fusion = bf16[2,192,48,192]{3,1,2,0:T(8,128)(2,1)} fusion(f32[192,48,192]{2,0,1:T(8,128)} %add_divide_fusion, bf16[2,192,48,192]{3,2,1,0:T(8,128)(2,1)} %bitcast.100, f32[192]{0:T(256)S(1)} %get-tuple-element.18, f32[192]{0:T(256)S(1)} %get-tuple-element.19), kind=kOutput, calls=%fused_computation.40 | convolution fusion | flops 2728747008 | bytes 21235200 | tf_op jit(solution)/shard_map/pxyz,kx->pkyz/dot_general | solution.py:67
  417.4 4.1 slice_bitcast_fusion.3
  421.6 5.7 pad_maximum_fusion.1
  427.3 59.7 %all-to-all-done = bf16[2,48,192,192]{3,1,0,2:T(8,128)(2,1)} async-done(((bf16[2,48,192,192]{3,1,0,2:T(8,128)(2,1)}), bf16[2,48,192,192]{3,1,0,2:T(8,128)(2,1)}, u32[]{:S(2)}, u32[]{:S(2)}) %all-to-all-start) | async-done | bytes 7077920 | tf_op jit(solution)/shard_map/all_to_all | solution.py:62
  487.0 6.2 all-to-all-start.3
  493.2 12.7 %copy.72 = bf16[2,4,48,48,192]{4,3,2,1,0:T(8,128)(2,1)} copy(bf16[2,4,48,48,192]{4,2,0,3,1:T(8,128)(2,1)} %bitcast.8) | data formatting | bytes 14155776 | tf_op jit(solution)/shard_map/all_to_all | solution.py:62
  505.9 16.1 %convert_bitcast_fusion.2 = bf16[2,192,48,192]{3,1,2,0:T(8,128)(2,1)} fusion(f32[192,48,192]{2,0,1:T(8,128)} %add_divide_fusion, bf16[2,192,48,192]{3,2,1,0:T(8,128)(2,1)} %bitcast.99, f32[192]{0:T(256)S(1)} %get-tuple-element.18, f32[192]{0:T(256)S(1)} %get-tuple-element.19), kind=kOutput, calls=%fused_computation.45 | convolution fusion | flops 2728747008 | bytes 21235200 | tf_op jit(solution)/shard_map/pxyz,kx->pkyz/dot_general | solution.py:67
  522.1 4.1 slice_bitcast_fusion.7
  526.2 5.8 pad_maximum_fusion
  532.0 64.4 %all-to-all-done.3 = bf16[4,2,48,48,192]{4,2,3,1,0:T(8,128)(2,1)} async-done(((bf16[4,2,48,48,192]{4,2,3,1,0:T(8,128)(2,1)}), bf16[4,2,48,48,192]{4,2,3,1,0:T(8,128)(2,1)}, u32[]{:S(2)}, u32[]{:S(2)}) %all-to-all-start.3) | async-done | bytes 7077920 | tf_op jit(solution)/shard_map/all_to_all | solution.py:12
  596.3 6.0 all-to-all-start.1
  602.3 10.9 copy.84
  613.3 13.7 %fusion.21 = f32[2,48,192,192]{3,2,1,0:T(8,128)} fusion(bf16[2,48,192,192]{3,2,1,0:T(8,128)(2,1)} %bitcast.102, f32[192]{0:T(256)S(1)} %get-tuple-element.18, f32[192]{0:T(256)S(1)} %get-tuple-element.19), kind=kOutput, calls=%fused_computation.31 | convolution fusion | flops 2721669120 | bytes 21235200 | tf_op jit(solution)/shard_map/dot_general | solution.py:76
  627.0 78.4 %all-to-all-done.1 = bf16[4,2,48,48,192]{4,2,3,1,0:T(8,128)(2,1)} async-done(((bf16[4,2,48,48,192]{4,2,3,1,0:T(8,128)(2,1)}), bf16[4,2,48,48,192]{4,2,3,1,0:T(8,128)(2,1)}, u32[]{:S(2)}, u32[]{:S(2)}) %all-to-all-start.1) | async-done | bytes 7077920 | tf_op jit(solution)/shard_map/all_to_all | solution.py:12
  705.5 11.0 copy.74
  716.5 34.3 %convert_multiply_fusion.2 = (f32[2,48,192,192]{3,2,1,0:T(8,128)}, f32[2,48,192,192]{3,2,1,0:T(8,128)}, f32[2,48,192,192]{3,2,1,0:T(8,128)}) fusion(bf16[2,48,192,192]{3,2,1,0:T(8,128)(2,1)} %param.2, f32[2,48,192,192]{3,2,1,0:T(8,128)} %fusion.21, f32[192]{0:T(256)S(1)} %get-tuple-element.18, f32[192]{0:T(256)S(1)} %get-tuple-element.19, ...), kind=kOutput, calls=%fused_computation.2 | convolution fusion | flops 2732285952 | bytes 70780416 | tf_op jit(solution)/shard_map/dot_general | solution.py:76
  750.7 59.0 %fusion.9 = bf16[2,48,192,192]{3,0,2,1:T(2,128)(2,1)} fusion(f32[2,48,192,192]{3,2,1,0:T(8,128)} %get-tuple-element.5, s32[2]{0:T(128)S(1)} %get-tuple-element.16), kind=kOutput, calls=%fused_computation.21 | convolution fusion | flops 84934656 | bytes 21233672 | tf_op jit(solution)/shard_map/ip,ixyz->pxyz/dot_general | solution.py:79
  809.7 0.0 copy-start.2
  809.7 9.3 copy.133
  819.0 0.0 copy-done.2
  819.0 58.8 %fusion.7 = bf16[2,48,192,192]{3,0,2,1:T(2,128)(2,1)} fusion(f32[2,48,192,192]{3,2,1,0:T(8,128)} %get-tuple-element.6, s32[2]{0:T(128)S(1)} %copy-done.2), kind=kOutput, calls=%fused_computation.19 | convolution fusion | flops 84934656 | bytes 21233672 | tf_op jit(solution)/shard_map/ip,ixyz->pxyz/dot_general | solution.py:79
  877.8 9.2 copy.132
  887.0 0.3 collective-permute-start.3
  887.3 0.0 collective-permute-start.1
  887.3 207.8 %collective-permute-done.3 = bf16[2,48,192,192]{3,2,1,0:T(8,128)(2,1)S(1)} collective-permute-done((bf16[2,48,192,192]{3,2,1,0:T(8,128)(2,1)}, bf16[2,48,192,192]{3,2,1,0:T(8,128)(2,1)S(1)}, u32[]{:S(2)}, u32[]{:S(2)}) %collective-permute-start.3) | collective-permute-done | bytes 7077920 | tf_op jit(solution)/shard_map/ppermute | solution.py:19
  1095.1 99.5 %collective-permute-done.1 = bf16[2,48,192,192]{3,2,1,0:T(8,128)(2,1)S(1)} collective-permute-done((bf16[2,48,192,192]{3,2,1,0:T(8,128)(2,1)}, bf16[2,48,192,192]{3,2,1,0:T(8,128)(2,1)S(1)}, u32[]{:S(2)}, u32[]{:S(2)}) %collective-permute-start.1) | collective-permute-done | bytes 7077920 | tf_op jit(solution)/shard_map/ppermute | solution.py:19
  1194.7 22.5 %fusion.4 = bf16[2,48,192,192]{3,2,1,0:T(8,128)(2,1)} fusion(f32[2,48,192,192]{3,2,1,0:T(8,128)} %get-tuple-element.17, f32[2,48,192,192]{3,2,1,0:T(8,128)} %fusion.21, bf16[2,48,192,192]{3,2,1,0:T(8,128)(2,1)S(1)} %collective-permute-done.3, bf16[2,48,192,192]{3,2,1,0:T(8,128)(2,1)S(1)} %collective-permute-done.1, bf16[2,48,192,192]{3,0,2,1:T(2,128)(2,1)} %fusion.123, ...), kind=kLoop, calls=%fused_computation.10 | loop fusion | flops 38928384 | bytes 63700992 | tf_op jit(solution)/shard_map/convert_element_type | solution.py:86
  (4 shorter events, 0.1 us)
Async XLA Ops:
  0.0 23.4 %copy-start = (s32[2,2]{1,0:T(2,128)S(1)}, s32[2,2]{1,0:T(2,128)}, u32[]{:S(2)}) copy-start(s32[2,2]{1,0:T(2,128)} %param.3) | copy-start | bytes 52
  18.3 207.6 %collective-permute-start.2 = (bf16[2,48,192,192]{3,0,2,1:T(2,128)(2,1)}, bf16[2,48,192,192]{3,0,2,1:T(2,128)(2,1)S(1)}, u32[]{:S(2)}, u32[]{:S(2)}) collective-permute-start(bf16[2,48,192,192]{3,0,2,1:T(2,128)(2,1)} %copy.67), channel_id=1, source_target_pairs={{8,0},{12,4},{16,8},{20,12},{24,16},{28,20},{0,24},{4,28},{9,1},{1... | collective-permute-start | bytes 21233672 | tf_op jit(solution)/shard_map/ppermute | solution.py:19
  23.4 303.6 %collective-permute-start = (bf16[2,48,192,192]{3,0,2,1:T(2,128)(2,1)}, bf16[2,48,192,192]{3,0,2,1:T(2,128)(2,1)}, u32[]{:S(2)}, u32[]{:S(2)}) collective-permute-start(bf16[2,48,192,192]{3,0,2,1:T(2,128)(2,1)} %copy.67), channel_id=1, source_target_pairs={{4,0},{8,4},{12,8},{16,12},{20,16},{24,20},{28,24},{0,28},{5,1},{9... | collective-permute-start | bytes 21233672 | tf_op jit(solution)/shard_map/ppermute | solution.py:19
  23.5 217.0 %copy-start.1 = (s32[2]{0:T(128)}, s32[2]{0:T(128)S(1)}, u32[]{:S(2)}) copy-start(s32[2]{0:T(128)S(1)} %get-tuple-element.15) | copy-start | bytes 28
  268.5 109.3 %all-to-all-start.2 = ((bf16[2,48,192,192]{3,1,0,2:T(8,128)(2,1)}), bf16[2,48,192,192]{3,1,0,2:T(8,128)(2,1)}, u32[]{:S(2)}, u32[]{:S(2)}) async-start(bf16[2,48,192,192]{3,1,0,2:T(8,128)(2,1)} %copy.80), calls=%async_computation.2 | async-start | bytes 18874368 | tf_op jit(solution)/shard_map/all_to_all | solution.py:62
  377.8 109.2 %all-to-all-start = ((bf16[2,48,192,192]{3,1,0,2:T(8,128)(2,1)}), bf16[2,48,192,192]{3,1,0,2:T(8,128)(2,1)}, u32[]{:S(2)}, u32[]{:S(2)}) async-start(bf16[2,48,192,192]{3,1,0,2:T(8,128)(2,1)} %copy.70), calls=%async_computation | async-start | bytes 18874368 | tf_op jit(solution)/shard_map/all_to_all | solution.py:62
  487.0 109.4 %all-to-all-start.3 = ((bf16[4,2,48,48,192]{4,2,3,1,0:T(8,128)(2,1)}), bf16[4,2,48,48,192]{4,2,3,1,0:T(8,128)(2,1)}, u32[]{:S(2)}, u32[]{:S(2)}) async-start(bf16[4,2,48,48,192]{4,2,3,1,0:T(8,128)(2,1)} %pad_maximum_fusion.1), calls=%async_computation.3 | async-start | bytes 18874368 | tf_op jit(solution)/shard_map/all_to_all | solution.py:12
  596.3 109.1 %all-to-all-start.1 = ((bf16[4,2,48,48,192]{4,2,3,1,0:T(8,128)(2,1)}), bf16[4,2,48,48,192]{4,2,3,1,0:T(8,128)(2,1)}, u32[]{:S(2)}, u32[]{:S(2)}) async-start(bf16[4,2,48,48,192]{4,2,3,1,0:T(8,128)(2,1)} %pad_maximum_fusion), calls=%async_computation.1 | async-start | bytes 18874368 | tf_op jit(solution)/shard_map/all_to_all | solution.py:12
  809.7 9.3 copy-start.2
  887.0 208.1 %collective-permute-start.3 = (bf16[2,48,192,192]{3,2,1,0:T(8,128)(2,1)}, bf16[2,48,192,192]{3,2,1,0:T(8,128)(2,1)S(1)}, u32[]{:S(2)}, u32[]{:S(2)}) collective-permute-start(bf16[2,48,192,192]{3,2,1,0:T(8,128)(2,1)} %copy.132), channel_id=1, source_target_pairs={{24,0},{28,4},{0,8},{4,12},{8,16},{12,20},{16,24},{20,28},{25,1},{... | collective-permute-start | bytes 21233672 | tf_op jit(solution)/shard_map/ppermute | solution.py:19
  887.3 307.4 %collective-permute-start.1 = (bf16[2,48,192,192]{3,2,1,0:T(8,128)(2,1)}, bf16[2,48,192,192]{3,2,1,0:T(8,128)(2,1)S(1)}, u32[]{:S(2)}, u32[]{:S(2)}) collective-permute-start(bf16[2,48,192,192]{3,2,1,0:T(8,128)(2,1)} %copy.133), channel_id=1, source_target_pairs={{28,0},{0,4},{4,8},{8,12},{12,16},{16,20},{20,24},{24,28},{29,1},{... | collective-permute-start | bytes 21233672 | tf_op jit(solution)/shard_map/ppermute | solution.py:19
